TPU v7x, 32 devices: a whole 2x2x4 slice. The times are simulated.
32 devices in a mesh: dp: 8 (over z, x), hyper: 4 (over y, core).
Axes of the slice: x: 2, y: 2, z: 4, core: 2. Of those that a mesh axis runs over, the one named last changes fastest.
Arguments:
- inputs: bfloat16 [64, 64, 128], P(('dp', 'hyper')), may hold values from -64 to 64
- labels: int32 [64, 64], P(('dp', 'hyper')), may hold values from 0 to 255
- client_ids: int32 [64], P(('dp', 'hyper')), may hold values from 0 to 63
- ext_weight: bfloat16 [128, 4096], replicated, may hold values from -0.5 to 0.5
- ext_bias: bfloat16 [4096], replicated, may hold values from -3 to 3
- embeddings: bfloat16 [64, 128], replicated, may hold values from -1.5 to 1.5
- hyper_in: bfloat16 [128, 50], replicated, may hold values from -2.09375 to 2.09375
- hyper_bias: float32 [50], replicated, may hold values from -3 to 3
- hyper_out: bfloat16 [4096, 50, 256], P('hyper'), may hold values from -0.1796875 to 0.1796875
Outputs:
- grad_ext_weight: float32 [128, 4096], replicated
- grad_ext_bias: float32 [4096], replicated
- grad_embeddings: float32 [64, 128], replicated
- grad_hyper_in: float32 [128, 50], replicated
- grad_hyper_bias: float32 [50], replicated
- grad_hyper_out: float32 [4096, 50, 256], P(('hyper', 'dp'))
Inputs may be any that keep to these rules, and one draw needn't show every extreme that they name: `client_ids`: A client may hold several slots or none.
All inputs are finite; a program needn't handle non-finite values.
Results may differ from a plain program's by a relative error of at most 0.014.
The roundings to bfloat16 on the way count: a program that leaves them out, or rounds other values in their place, can miss the bound.
Values may be sent and summed in bfloat16 or wider, within the bound.
A program may use at most 192 MiB of HBM per device.

v0:
```python
import jax
import jax.numpy as jnp
from jax import lax
from jax.sharding import PartitionSpec as P

highest = lax.Precision.HIGHEST
f32 = jnp.float32
bf16 = jnp.bfloat16


def silu_slope(values):
    logistic = jax.nn.sigmoid(values)
    return logistic * (1.0 + values * (1.0 - logistic))


def class_grads(logits, slot_labels, row_count):
    largest = jnp.max(logits, axis=-1, keepdims=True)
    exponent = jnp.exp(logits - largest)
    probability = exponent / jnp.sum(exponent, axis=-1, keepdims=True)
    classes = jnp.arange(logits.shape[-1], dtype=jnp.int32)
    onehot = (slot_labels[..., None] == classes).astype(f32)
    return ((probability - onehot) / row_count).astype(bf16)


def local(
    inputs, labels, client_ids, ext_weight, ext_bias, embeddings, hyper_in, hyper_bias, hyper_out
):
    everyone = ("dp", "hyper")
    n_dp, n_hyper = (lax.axis_size("dp"), lax.axis_size("hyper"))
    i, j = (lax.axis_index("dp"), lax.axis_index("hyper"))
    own, rows, width_in = inputs.shape
    wide = hyper_out.shape[0]
    narrow = wide // n_dp
    group = own * n_hyper
    slots = group * n_dp
    classes = hyper_out.shape[2]
    ids = lax.all_gather(client_ids, everyone, axis=0, tiled=True)
    in_group = lax.all_gather(inputs, "hyper", axis=0, tiled=True)
    in_all = lax.all_gather(in_group, "dp", axis=0, tiled=True)
    select = ids[:, None] == jnp.arange(embeddings.shape[0], dtype=jnp.int32)[None, :]
    picked = jnp.dot(select.astype(bf16), embeddings, preferred_element_type=f32).astype(bf16)
    hyper_preact = jnp.dot(picked, hyper_in, preferred_element_type=f32) + hyper_bias
    hidden = jax.nn.silu(hyper_preact).astype(bf16)
    w_wide = lax.dynamic_slice_in_dim(ext_weight, j * wide, wide, 1)
    b_wide = lax.dynamic_slice_in_dim(ext_bias, j * wide, wide, 0).astype(f32)
    preact = jnp.dot(in_group.reshape(group * rows, width_in), w_wide, preferred_element_type=f32)
    features = jax.nn.silu(preact + b_wide).astype(bf16).reshape(group, rows, wide)
    hidden_group = lax.dynamic_slice_in_dim(hidden, i * group, group, 0)
    heads = jnp.einsum("kh,dhc->kdc", hidden_group, hyper_out, preferred_element_type=f32)
    part = jnp.einsum("krd,kdc->krc", features, heads.astype(bf16), preferred_element_type=f32)
    parts = lax.all_to_all(
        part.reshape(n_hyper, own * rows, classes), "hyper", split_axis=0, concat_axis=0
    )
    logits = jnp.sum(parts, axis=0).reshape(own, rows, classes)
    dlogits = class_grads(logits, labels, rows)
    dl_all = lax.all_gather(dlogits, everyone, axis=0, tiled=True)
    start = (j * n_dp + i) * narrow
    w = lax.dynamic_slice_in_dim(ext_weight, start, narrow, 1)
    b = lax.dynamic_slice_in_dim(ext_bias, start, narrow, 0).astype(f32)
    out_rows = lax.dynamic_slice_in_dim(hyper_out, i * narrow, narrow, 0)
    flat = in_all.reshape(slots * rows, width_in)
    preact = jnp.dot(flat, w, preferred_element_type=f32) + b
    features = jax.nn.silu(preact).astype(bf16).reshape(slots, rows, narrow)
    heads = jnp.einsum("kh,dhc->kdc", hidden, out_rows, preferred_element_type=f32).astype(bf16)
    dheads = jnp.einsum("krd,krc->kdc", features, dl_all, preferred_element_type=f32).astype(bf16)
    dfeatures = jnp.einsum("krc,kdc->krd", dl_all, heads, preferred_element_type=f32).astype(bf16)
    dpreact = (dfeatures.reshape(slots * rows, narrow).astype(f32) * silu_slope(preact)).astype(
        bf16
    )
    grad_weight = jnp.dot(flat.T, dpreact, preferred_element_type=f32)
    grad_bias = jnp.sum(dpreact.astype(f32), axis=0)
    grad_out = jnp.einsum("kh,kdc->dhc", hidden, dheads, preferred_element_type=f32)
    dhidden = jnp.einsum("kdc,dhc->kh", dheads, out_rows, preferred_element_type=f32)
    dhidden = lax.psum(dhidden, everyone)
    hyper_dpre = dhidden * silu_slope(hyper_preact)
    grad_in = jnp.dot(picked.astype(f32).T, hyper_dpre, precision=highest)
    grad_hbias = jnp.sum(hyper_dpre, axis=0)
    back_rows = jnp.dot(hyper_dpre, hyper_in.astype(f32).T, precision=highest)
    grad_table = jnp.dot(select.astype(f32).T, back_rows, precision=highest)
    both = jnp.concatenate([grad_weight, grad_bias[None]], axis=0)
    both = lax.all_gather(both, ("hyper", "dp"), axis=1, tiled=True)
    return (both[:-1], both[-1], grad_table, grad_in, grad_hbias, grad_out)


def solution(mesh):
    placed = (
        P(("dp", "hyper"), None, None),
        P(("dp", "hyper"), None),
        P(("dp", "hyper")),
        P(),
        P(),
        P(),
        P(),
        P(),
        P("hyper", None, None),
    )
    return jax.shard_map(
        local,
        mesh=mesh,
        in_specs=placed,
        out_specs=(P(), P(), P(), P(), P(), P(("hyper", "dp"), None, None)),
        check_vma=False,
    )
```

profile of v0, /device:TPU:0, one launch (start us, length us, event | category | flops | bytes accessed | tf_op | source)
XLA Modules:
  0.0 276.0 jit_solution(7571744221663631513)
XLA Ops:
  7.2 0.9 dynamic-update-slice
  8.2 42.0 %all-reduce = s32[64]{0:T(128)S(1)} all-reduce(s32[64]{0:T(128)S(1)} %dynamic-update-slice), channel_id=1, replica_groups=mesh['dp'=8,'hyper'=4] {'dp','hyper'}, use_global_device_ids=true, to_apply=%add | all-reduce | flops 64 | bytes 512
  50.1 6.0 %all_gather.15 = bf16[8,64,128]{2,1,0:T(8,128)(2,1)S(1)} all-gather(bf16[2,64,128]{2,1,0:T(8,128)(2,1)} %param.9), channel_id=1, replica_groups=mesh['dp'=8,'hyper'=4] {'hyper'}, dimensions={0}, use_global_device_ids=true | all-gather | bytes 163840 | tf_op jit(solution)/shard_map/all_gather | solution.py:38
  56.8 0.9 convolution_convert_fusion.2
  57.7 0.9 multiply_convert_fusion.3
  59.4 28.0 %convolution_convert_fusion.1 = bf16[8,1024,256]{2,0,1:T(8,128)(2,1)S(1)} fusion(bf16[64,50]{0,1:T(8,128)(2,1)S(1)} %get-tuple-element.29, s32[]{:T(128)S(6)} %select_n.15, bf16[1024,50,256]{2,0,1:T(8,128)(2,1)} %param.17), kind=kOutput, calls=%fused_computation.16 | convolution fusion | flops 211812352 | bytes 30415108 | tf_op jit(solution)/shard_map/kh,dhc->kdc/dot_general | solution.py:49
  87.4 0.9 fusion.3
  88.2 11.8 %all_to_all.5 = f32[4,128,256]{2,1,0:T(8,128)S(1)} all-to-all(f32[4,128,256]{2,1,0:T(8,128)S(1)} %bitcast.61), channel_id=1, replica_groups=mesh['dp'=8,'hyper'=4] {'hyper'}, dimensions={0} | all-to-all | bytes 1048576 | tf_op jit(solution)/shard_map/all_to_all | solution.py:51
  102.1 27.8 %copy.28 = bf16[1024,50,256]{2,1,0:T(8,128)(2,1)} copy(bf16[1024,50,256]{2,0,1:T(8,128)(2,1)} %param.17) | data formatting | bytes 52428800 | tf_op args[8]
  130.6 5.3 %fusion.15 = bf16[64,128,256]{2,0,1:T(8,128)(2,1)} fusion(bf16[1024,50,256]{2,1,0:T(8,128)(2,1)} %copy.28, s32[]{:T(128)S(6)} %select_n.16, bf16[64,50]{0,1:T(8,128)(2,1)S(1)} %get-tuple-element.29), kind=kOutput, calls=%fused_computation.14 | convolution fusion | flops 211812352 | bytes 7870724 | tf_op jit(solution)/shard_map/kh,dhc->kdc/dot_general | solution.py:64
  136.0 20.6 %all-gather.4.cloned.1.call-done = bf16[64,64,256]{2,1,0:T(8,128)(2,1)} async-done(((bf16[2,64,256]{2,1,0:T(8,128)(2,1)}), bf16[64,64,256]{2,1,0:T(8,128)(2,1)}) %all-gather.4.cloned.1.call-update) | async-done | bytes 2097168 | tf_op jit(solution)/shard_map/all_gather | solution.py:56
  156.5 5.5 %fusion.22 = bf16[64,64,128]{2,1,0:T(8,128)(2,1)S(1)} fusion(bf16[64,64,256]{2,1,0:T(8,128)(2,1)} %all-gather.4.cloned.1.call-done, bf16[64,128,256]{2,0,1:T(8,128)(2,1)} %fusion.15), kind=kOutput, calls=%fused_computation.27 | convolution fusion | flops 268959744 | bytes 7340032 | tf_op jit(solution)/shard_map/krc,kdc->krd/dot_general | solution.py:66
  162.3 1.8 copy.32
  164.1 33.7 %all-gather.6.cloned.1.call-done = bf16[64,64,128]{2,1,0:T(8,128)(2,1)} async-done(((bf16[8,64,128]{2,1,0:T(8,128)(2,1)}), bf16[64,64,128]{2,1,0:T(8,128)(2,1)}) %all-gather.6.cloned.1.call-update) | async-done | bytes 1048592 | tf_op jit(solution)/shard_map/all_gather | solution.py:39
  197.8 4.2 %convert_reduce_fusion = (f32[128]{0:T(128)S(1)}, bf16[4096,128]{0,1:T(8,128)(2,1)S(1)}, bf16[4096,128]{0,1:T(8,128)(2,1)}) fusion(f32[4096,128]{0,1:T(8,128)} %copy.32, f32[128]{0:T(128)S(1)} %dynamic-slice_convert_fusion.1, bf16[4096,128]{1,0:T(8,128)(2,1)} %bitcast.58, bf16[128,4096]{1,0:T(8,128)(2,1)S(1)} %copy-done, s32[]{:T(128)S(6)} %select_n.17), kind=kOutput, calls=%fused_computation.23 | convolution fusion | flops 141557632 | bytes 5276676 | tf_op jit(solution)/shard_map/dot_general | solution.py:62
  203.2 2.3 copy.33
  205.5 2.5 convolution_convert_fusion
  208.0 3.3 %fusion.12 = f32[128,50,256]{2,1,0:T(8,128)S(1)} fusion(bf16[64,128,256]{2,1,0:T(8,128)(2,1)S(1)} %convolution_convert_fusion, bf16[64,50]{0,1:T(8,128)(2,1)S(1)} %get-tuple-element.29), kind=kOutput, calls=%fused_computation.13 | convolution fusion | flops 209715200 | bytes 10754304 | tf_op jit(solution)/shard_map/kh,kdc->dhc/dot_general | solution.py:72
  211.3 4.8 %copy.37 = f32[128,50,256]{2,0,1:T(8,128)} copy(f32[128,50,256]{2,1,0:T(8,128)S(1)} %fusion.12) | data formatting | bytes 13107200
  216.1 7.1 %fusion.25 = f32[64,50]{0,1:T(8,128)S(1)} fusion(bf16[1024,50,256]{2,1,0:T(8,128)(2,1)} %copy.28, s32[]{:T(128)S(6)} %select_n.16, bf16[64,128,256]{2,1,0:T(8,128)(2,1)S(1)} %convolution_convert_fusion), kind=kOutput, calls=%fused_computation.29 | convolution fusion | flops 209715200 | bytes 7877124 | tf_op jit(solution)/shard_map/kdc,dhc->kh/dot_general | solution.py:73
  223.2 39.1 %psum.7 = f32[64,50]{0,1:T(8,128)S(1)} all-reduce(f32[64,50]{0,1:T(8,128)S(1)} %fusion.25), channel_id=1, replica_groups=mesh['dp'=8,'hyper'=4] {'dp','hyper'}, use_global_device_ids=true, to_apply=%region_4.5 | all-reduce | flops 3200 | bytes 25600 | tf_op jit(solution)/shard_map/psum | solution.py:74
  263.2 0.9 fusion.32
  264.9 1.5 slice.9
  266.4 3.1 %slice.8 = f32[128,4096]{1,0:T(8,128)} slice(f32[129,4096]{1,0:T(8,128)} %all-gather.8.cloned.1.call-done), slice={[0:128], [0:4096]} | slice | bytes 4194304 | tf_op jit(solution)/shard_map/slice | solution.py:82
  (35 shorter events, 7.3 us)
Async XLA Ops:
  7.2 51.5 %copy-start = (bf16[128,4096]{1,0:T(8,128)(2,1)S(1)}, bf16[128,4096]{1,0:T(8,128)(2,1)}, u32[]{:S(2)}) copy-start(bf16[128,4096]{1,0:T(8,128)(2,1)} %param.12) | copy-start | bytes 3145732
  7.2 149.4 %all-gather.4.cloned.1.call-start = ((), (), s32[]{:S(2)}) async-start(), calls=%async_computation.1 | async-start | bytes 2162688 | tf_op jit(solution)/shard_map/all_gather | solution.py:56
  56.1 3.2 %copy-start.3 = (bf16[8,64,128]{2,1,0:T(8,128)(2,1)}, bf16[8,64,128]{2,1,0:T(8,128)(2,1)S(1)}, u32[]{:S(2)}) copy-start(bf16[8,64,128]{2,1,0:T(8,128)(2,1)S(1)} %all_gather.15) | copy-start | bytes 393220
  87.4 13.1 %copy-start.5 = (s32[2,64]{1,0:T(2,128)S(1)}, s32[2,64]{1,0:T(2,128)}, u32[]{:S(2)}) copy-start(s32[2,64]{1,0:T(2,128)} %param.10) | copy-start | bytes 1540
  101.3 96.5 %all-gather.6.cloned.1.call-start = ((), (), s32[]{:S(2)}) async-start(), calls=%async_computation.2 | async-start | bytes 1179648 | tf_op jit(solution)/shard_map/all_gather | solution.py:39
  102.0 162.8 %all-gather.8.cloned.1.call-start = ((), (), s32[]{:S(2)}) async-start(), calls=%async_computation.3 | async-start | bytes 2297856 | tf_op jit(solution)/shard_map/all_gather | solution.py:81
  197.8 4.2 %copy-start.2 = (bf16[64,64,128]{2,1,0:T(8,128)(2,1)S(1)}, bf16[64,64,128]{2,1,0:T(8,128)(2,1)}, u32[]{:S(2)}) copy-start(bf16[64,64,128]{2,1,0:T(8,128)(2,1)} %all-gather.6.cloned.1.call-done) | copy-start | bytes 3145732
  202.1 3.4 %copy-start.1 = (bf16[64,64,256]{2,1,0:T(8,128)(2,1)S(1)}, bf16[64,64,256]{2,1,0:T(8,128)(2,1)}, u32[]{:S(2)}) copy-start(bf16[64,64,256]{2,1,0:T(8,128)(2,1)} %all-gather.4.cloned.1.call-done) | copy-start | bytes 6291460
  216.1 46.9 %copy-start.4 = (bf16[128,50]{0,1:T(8,128)(2,1)S(1)}, bf16[128,50]{0,1:T(8,128)(2,1)}, u32[]{:S(2)}) copy-start(bf16[128,50]{0,1:T(8,128)(2,1)} %param.15) | copy-start | bytes 38404
Sparse Core Ops, SparseCore 0:
  101.4 55.0 all-gather.3
  158.7 39.1 all-gather.5
  203.4 56.2 all-gather.7
where the time goes:
time: 277 us; the launch traced here: 276 us
  blocking collectives  98.8 us (36%)
  matrix products  61.7 us (22%)
  waiting for transfers between devices  55.1 us (20%)
  local copies, waits for them, and re-layouts  42.4 us (15%)
  between operations  13.9 us (5%)
  other arithmetic  4 us (1%)
    unnamed x1, blocking collectives  42 us
    psum x1, blocking collectives, local(): dhidden = lax.psum(dhidden, everyone)  39.1 us
    all_gather x1, waiting for transfers between devices, local(): in_all = lax.all_gather(in_group, 'dp', axis=0, tiled=True)  33.7 us
    unnamed x16, local copies, waits for them, and re-layouts  33.5 us
    dot_general x1, matrix products, local(): jnp.einsum('kh,dhc->kdc', hidden_group, hyper_out, preferred_element_type...  28 us
    all_gather x1, waiting for transfers between devices, local(): dl_all = lax.all_gather(dlogits, everyone, axis=0, tiled=True)  20.6 us
    all_to_all x1, blocking collectives, local(): lax.all_to_all(part.reshape(n_hyper, own * rows, classes), 'hyper', split...  11.8 us
    dot_general x1, matrix products, local(): jnp.einsum('kdc,dhc->kh', dheads, out_rows, preferred_element_type=f32)  7.1 us
  transfers between devices with their start and end apart: 3, of which 2 were waited for; matrix products, arithmetic and copies ran while one was open for 23% of the time, Pallas kernels for 0%

commit v1 on v0

--- a/solution.py
+++ b/solution.py
@@ -6,6 +6,12 @@
 highest = lax.Precision.HIGHEST
 f32 = jnp.float32
 bf16 = jnp.bfloat16
+
+
+def joined_along(tiles, dim):
+    tiles = jnp.moveaxis(tiles, 0, dim)
+    dims = tiles.shape
+    return tiles.reshape(*dims[:dim], dims[dim] * dims[dim + 1], *dims[dim + 2 :])
 
 
 def silu_slope(values):
@@ -36,7 +42,14 @@
     classes = hyper_out.shape[2]
     ids = lax.all_gather(client_ids, everyone, axis=0, tiled=True)
     in_group = lax.all_gather(inputs, "hyper", axis=0, tiled=True)
-    in_all = lax.all_gather(in_group, "dp", axis=0, tiled=True)
+    length = lax.axis_size("dp")
+    right = [(i_2, (i_2 + 1) % length) for i_2 in range(length)]
+    parts_2 = [in_group]
+    while len(parts_2) < length:
+        parts_2.append(lax.ppermute(parts_2[-1], "dp", right))
+    here = lax.axis_index("dp")
+    parts_2 = jnp.stack(parts_2)[(here - jnp.arange(length)) % length]
+    in_all = joined_along(parts_2, 0)
     select = ids[:, None] == jnp.arange(embeddings.shape[0], dtype=jnp.int32)[None, :]
     picked = jnp.dot(select.astype(bf16), embeddings, preferred_element_type=f32).astype(bf16)
     hyper_preact = jnp.dot(picked, hyper_in, preferred_element_type=f32) + hyper_bias

time: 277 us -> 255 us (0.921)
  local copies, waits for them, and re-layouts: 42.4 us -> 26.5 us
  waiting for transfers between devices: 55.1 us -> 49.5 us
  starting transfers between devices: 0.12 us -> 3.16 us
  matrix products: 61.7 us -> 58.7 us
    ppermute x0 -> x7, waiting for transfers between devices: none -> 49.4 us  [local(): parts_2.append(lax.ppermute(parts_2[-1], 'dp', right))]
    all_gather x1 -> x0, waiting for transfers between devices: 33.7 us -> none  [local(): in_all = lax.all_gather(in_group, 'dp', axis=0, tiled=True)]
    unnamed x16 -> x29, local copies, waits for them, and re-layouts: 33.5 us -> 12.3 us
    all_gather x1, waiting for transfers between devices: 20.6 us -> 0.02 us  [local(): dl_all = lax.all_gather(dlogits, everyone, axis=0, tiled=True)]
    dot_general x1, matrix products: 7.1 us -> 1.26 us  [local(): jnp.einsum('kdc,dhc->kh', dheads, out_rows, preferred_element_type=f32)]
    ppermute x0 -> x7, starting transfers between devices: none -> 3.08 us  [local(): parts_2.append(lax.ppermute(parts_2[-1], 'dp', right))]
    convert_element_type x2 -> x1, local copies, waits for them, and re-layouts: 4.08 us -> 6.53 us  [local(): jnp.einsum('krd,krc->kdc', features, dl_all, preferred_element_type=f32)]
  transfers between devices with their start and end apart: 3 -> 9, of which waited for: 2 -> 6; matrix products, arithmetic and copies ran while one was open for 23% -> 15% of each run, Pallas kernels for 0% -> 0%
where the time goes in v1:
time: 255 us; the launch traced here: 254 us
  blocking collectives  98.2 us (39%)
  matrix products  58.7 us (23%)
  waiting for transfers between devices  49.5 us (19%)
  local copies, waits for them, and re-layouts  26.5 us (10%)
  between operations  14.3 us (6%)
  other arithmetic  3.82 us (1%)
  starting transfers between devices  3.16 us (1%)
    ppermute x7, waiting for transfers between devices, local(): parts_2.append(lax.ppermute(parts_2[-1], 'dp', right))  49.4 us
    unnamed x1, blocking collectives  42 us
    psum x1, blocking collectives, local(): dhidden = lax.psum(dhidden, everyone)  38.5 us
    dot_general x1, matrix products, local(): jnp.einsum('kh,dhc->kdc', hidden_group, hyper_out, preferred_element_type...  27.9 us
    unnamed x29, local copies, waits for them, and re-layouts  12.3 us
    all_to_all x1, blocking collectives, local(): lax.all_to_all(part.reshape(n_hyper, own * rows, classes), 'hyper', split...  11.8 us
    convert_element_type x1, local copies, waits for them, and re-layouts, local(): jnp.einsum('krd,krc->kdc', features, dl_all, preferred_element_type=f32)  6.53 us
    all_gather x1, blocking collectives, local(): in_group = lax.all_gather(inputs, 'hyper', axis=0, tiled=True)  6.01 us
  transfers between devices with their start and end apart: 9, of which 6 were waited for; matrix products, arithmetic and copies ran while one was open for 15% of the time, Pallas kernels for 0%

profile of v1, /device:TPU:0, one launch (start us, length us, event | category | flops | bytes accessed | tf_op | source)
XLA Modules:
  0.0 254.1 jit_solution(4596444485275928330)
XLA Ops:
  8.2 42.0 %all-reduce = s32[64]{0:T(128)S(1)} all-reduce(s32[64]{0:T(128)S(1)} %dynamic-update-slice), channel_id=1, replica_groups=mesh['dp'=8,'hyper'=4] {'dp','hyper'}, use_global_device_ids=true, to_apply=%add | all-reduce | flops 64 | bytes 512
  50.1 6.0 %all_gather.12 = bf16[8,64,128]{2,1,0:T(8,128)(2,1)S(1)} all-gather(bf16[2,64,128]{2,1,0:T(8,128)(2,1)} %param.9), channel_id=1, replica_groups=mesh['dp'=8,'hyper'=4] {'hyper'}, dimensions={0}, use_global_device_ids=true | all-gather | bytes 163840 | tf_op jit(solution)/shard_map/all_gather | solution.py:44
  58.6 1.7 fusion.15
  60.3 27.9 %fusion = bf16[8,1024,256]{2,0,1:T(8,128)(2,1)S(1)} fusion(bf16[1024,50,256]{2,0,1:T(8,128)(2,1)} %param.17, bf16[64,50]{0,1:T(8,128)(2,1)S(1)} %get-tuple-element.23, s32[]{:T(128)S(6)} %select_n.41), kind=kOutput, calls=%fused_computation.1 | convolution fusion | flops 209715200 | bytes 30415108 | tf_op jit(solution)/shard_map/kh,dhc->kdc/dot_general | solution.py:62
  88.2 2.1 fusion.2
  90.3 11.8 %all_to_all.5 = f32[4,128,256]{2,1,0:T(8,128)S(1)} all-to-all(f32[4,128,256]{2,1,0:T(8,128)S(1)} %bitcast.78), channel_id=1, replica_groups=mesh['dp'=8,'hyper'=4] {'hyper'}, dimensions={0} | all-to-all | bytes 1048576 | tf_op jit(solution)/shard_map/all_to_all | solution.py:64
  104.8 2.2 constant_dynamic-slice_fusion
  107.0 5.1 %fusion.6 = bf16[64,128,256]{2,0,1:T(8,128)(2,1)} fusion(bf16[128,50,256]{2,0,1:T(8,128)(2,1)S(1)} %constant_dynamic-slice_fusion, bf16[64,50]{0,1:T(8,128)(2,1)S(1)} %get-tuple-element.23), kind=kOutput, calls=%fused_computation.10 | convolution fusion | flops 209715200 | bytes 7477504 | tf_op jit(solution)/shard_map/kh,dhc->kdc/dot_general | solution.py:77
  112.8 1.7 collective-permute-start.1
  114.5 6.5 %collective-permute-done.1 = bf16[8,64,128]{2,1,0:T(8,128)(2,1)S(1)} collective-permute-done((bf16[8,64,128]{2,1,0:T(8,128)(2,1)S(1)}, bf16[8,64,128]{2,1,0:T(8,128)(2,1)S(1)}, u32[]{:S(2)}, u32[]{:S(2)}) %collective-permute-start.1) | collective-permute-done | bytes 131104 | tf_op jit(solution)/shard_map/ppermute | solution.py:49
  121.1 7.6 %collective-permute-done.2 = bf16[8,64,128]{2,1,0:T(8,128)(2,1)S(1)} collective-permute-done((bf16[8,64,128]{2,1,0:T(8,128)(2,1)S(1)}, bf16[8,64,128]{2,1,0:T(8,128)(2,1)S(1)}, u32[]{:S(2)}, u32[]{:S(2)}) %collective-permute-start.2) | collective-permute-done | bytes 131104 | tf_op jit(solution)/shard_map/ppermute | solution.py:49
  128.7 8.2 %collective-permute-done.3 = bf16[8,64,128]{2,1,0:T(8,128)(2,1)S(1)} collective-permute-done((bf16[8,64,128]{2,1,0:T(8,128)(2,1)S(1)}, bf16[8,64,128]{2,1,0:T(8,128)(2,1)S(1)}, u32[]{:S(2)}, u32[]{:S(2)}) %collective-permute-start.3) | collective-permute-done | bytes 131104 | tf_op jit(solution)/shard_map/ppermute | solution.py:49
  136.9 7.8 %collective-permute-done.4 = bf16[8,64,128]{2,1,0:T(8,128)(2,1)S(1)} collective-permute-done((bf16[8,64,128]{2,1,0:T(8,128)(2,1)S(1)}, bf16[8,64,128]{2,1,0:T(8,128)(2,1)S(1)}, u32[]{:S(2)}, u32[]{:S(2)}) %collective-permute-start.4) | collective-permute-done | bytes 131104 | tf_op jit(solution)/shard_map/ppermute | solution.py:49
  144.8 11.7 %collective-permute-done.5 = bf16[8,64,128]{2,1,0:T(8,128)(2,1)S(1)} collective-permute-done((bf16[8,64,128]{2,1,0:T(8,128)(2,1)S(1)}, bf16[8,64,128]{2,1,0:T(8,128)(2,1)S(1)}, u32[]{:S(2)}, u32[]{:S(2)}) %collective-permute-start.5) | collective-permute-done | bytes 131104 | tf_op jit(solution)/shard_map/ppermute | solution.py:49
  156.4 7.6 %collective-permute-done.6 = bf16[8,64,128]{2,1,0:T(8,128)(2,1)S(1)} collective-permute-done((bf16[8,64,128]{2,1,0:T(8,128)(2,1)S(1)}, bf16[8,64,128]{2,1,0:T(8,128)(2,1)S(1)}, u32[]{:S(2)}, u32[]{:S(2)}) %collective-permute-start.6) | collective-permute-done | bytes 131104 | tf_op jit(solution)/shard_map/ppermute | solution.py:49
  164.9 5.5 %fusion.16 = bf16[64,64,128]{2,1,0:T(8,128)(2,1)S(1)} fusion(bf16[64,64,256]{2,1,0:T(8,128)(2,1)} %all-gather.3.cloned.1.call-done, bf16[64,128,256]{2,0,1:T(8,128)(2,1)} %fusion.6), kind=kOutput, calls=%fused_computation.25 | convolution fusion | flops 268959744 | bytes 7340032 | tf_op jit(solution)/shard_map/krc,kdc->krd/dot_general | solution.py:79
  170.4 2.3 convert_reduce_fusion
  173.9 6.4 %copy.27 = bf16[128,50,256]{0,1,2:T(8,128)(2,1)} copy(bf16[128,50,256]{2,0,1:T(8,128)(2,1)} %copy-done.2) | data formatting | bytes 6553600
  180.3 3.3 %convolution_convert_fusion = bf16[64,128,256]{2,1,0:T(8,128)(2,1)} fusion(bf16[64,64,128]{2,1,0:T(8,128)(2,1)S(1)} %bitcast.76, bf16[64,64,256]{2,1,0:T(8,128)(2,1)S(1)} %copy-done.5), kind=kOutput, calls=%fused_computation.13 | convolution fusion | flops 270532608 | bytes 7340032 | tf_op jit(solution)/shard_map/krd,krc->kdc/dot_general | solution.py:78
  183.6 6.5 %copy.20 = bf16[64,128,256]{1,0,2:T(8,128)(2,1)} copy(bf16[64,128,256]{2,1,0:T(8,128)(2,1)} %convolution_convert_fusion) | data formatting | bytes 8388608 | tf_op jit(solution)/shard_map/convert_element_type | solution.py:78
  190.1 5.4 %fusion.8 = f32[128,50,256]{2,1,0:T(8,128)S(1)} fusion(bf16[64,128,256]{2,1,0:T(8,128)(2,1)} %convolution_convert_fusion, bf16[64,50]{0,1:T(8,128)(2,1)S(1)} %get-tuple-element.23), kind=kOutput, calls=%fused_computation.12 | convolution fusion | flops 209715200 | bytes 10754304 | tf_op jit(solution)/shard_map/kh,kdc->dhc/dot_general | solution.py:85
  195.6 4.8 %copy.22 = f32[128,50,256]{2,0,1:T(8,128)} copy(f32[128,50,256]{2,1,0:T(8,128)S(1)} %fusion.8) | data formatting | bytes 13107200
  201.6 38.5 %psum.7 = f32[64,50]{0,1:T(8,128)S(1)} all-reduce(f32[64,50]{0,1:T(8,128)S(1)} %convolution_bitcast_fusion), channel_id=1, replica_groups=mesh['dp'=8,'hyper'=4] {'dp','hyper'}, use_global_device_ids=true, to_apply=%region_4.5 | all-reduce | flops 3200 | bytes 25600 | tf_op jit(solution)/shard_map/psum | solution.py:87
  244.2 3.1 %slice.10 = f32[128,4096]{1,0:T(8,128)} slice(f32[129,4096]{1,0:T(8,128)} %all-gather.5.cloned.1.call-done), slice={[0:128], [0:4096]} | slice | bytes 4194304 | tf_op jit(solution)/shard_map/slice | solution.py:95
  (62 shorter events, 14.3 us)
Async XLA Ops:
  7.2 51.5 %copy-start = (bf16[128,4096]{1,0:T(8,128)(2,1)S(1)}, bf16[128,4096]{1,0:T(8,128)(2,1)}, u32[]{:S(2)}) copy-start(bf16[128,4096]{1,0:T(8,128)(2,1)} %param.12) | copy-start | bytes 3145732
  7.2 157.7 %all-gather.3.cloned.1.call-start = ((), (), s32[]{:S(2)}) async-start(), calls=%async_computation.1 | async-start | bytes 2162688 | tf_op jit(solution)/shard_map/all_gather | solution.py:69
  88.2 14.4 %copy-start.8 = (s32[2,64]{1,0:T(2,128)S(1)}, s32[2,64]{1,0:T(2,128)}, u32[]{:S(2)}) copy-start(s32[2,64]{1,0:T(2,128)} %param.10) | copy-start | bytes 1540
  103.4 139.3 %all-gather.5.cloned.1.call-start = ((), (), s32[]{:S(2)}) async-start(), calls=%async_computation.2 | async-start | bytes 2297856 | tf_op jit(solution)/shard_map/all_gather | solution.py:94
  103.4 9.4 %collective-permute-start = (bf16[8,64,128]{2,1,0:T(8,128)(2,1)S(1)}, bf16[8,64,128]{2,1,0:T(8,128)(2,1)S(1)}, u32[]{:S(2)}, u32[]{:S(2)}) collective-permute-start(bf16[8,64,128]{2,1,0:T(8,128)(2,1)S(1)} %all_gather.12), channel_id=1, source_target_pairs={{0,4},{4,8},{8,12},{12,16},{16,20},{20,24},{24,28},{28,0},{1,5},{5... | collective-permute-start | bytes 393224 | tf_op jit(solution)/shard_map/ppermute | solution.py:49
  107.0 5.1 %copy-start.2 = (bf16[128,50,256]{2,0,1:T(8,128)(2,1)}, bf16[128,50,256]{2,0,1:T(8,128)(2,1)S(1)}, u32[]{:S(2)}) copy-start(bf16[128,50,256]{2,0,1:T(8,128)(2,1)S(1)} %constant_dynamic-slice_fusion) | copy-start | bytes 9830404
  112.8 8.2 %collective-permute-start.1 = (bf16[8,64,128]{2,1,0:T(8,128)(2,1)S(1)}, bf16[8,64,128]{2,1,0:T(8,128)(2,1)S(1)}, u32[]{:S(2)}, u32[]{:S(2)}) collective-permute-start(bf16[8,64,128]{2,1,0:T(8,128)(2,1)S(1)} %collective-permute-done), channel_id=1, source_target_pairs={{0,4},{4,8},{8,12},{12,16},{16,20},{20,24},{24,28},{28,0},{1,5},{5... | collective-permute-start | bytes 393224 | tf_op jit(solution)/shard_map/ppermute | solution.py:49
  121.0 7.7 %collective-permute-start.2 = (bf16[8,64,128]{2,1,0:T(8,128)(2,1)S(1)}, bf16[8,64,128]{2,1,0:T(8,128)(2,1)S(1)}, u32[]{:S(2)}, u32[]{:S(2)}) collective-permute-start(bf16[8,64,128]{2,1,0:T(8,128)(2,1)S(1)} %collective-permute-done.1), channel_id=1, source_target_pairs={{0,4},{4,8},{8,12},{12,16},{16,20},{20,24},{24,28},{28,0},{1,5},{5... | collective-permute-start | bytes 393224 | tf_op jit(solution)/shard_map/ppermute | solution.py:49
  128.7 8.2 %collective-permute-start.3 = (bf16[8,64,128]{2,1,0:T(8,128)(2,1)S(1)}, bf16[8,64,128]{2,1,0:T(8,128)(2,1)S(1)}, u32[]{:S(2)}, u32[]{:S(2)}) collective-permute-start(bf16[8,64,128]{2,1,0:T(8,128)(2,1)S(1)} %collective-permute-done.2), channel_id=1, source_target_pairs={{0,4},{4,8},{8,12},{12,16},{16,20},{20,24},{24,28},{28,0},{1,5},{5... | collective-permute-start | bytes 393224 | tf_op jit(solution)/shard_map/ppermute | solution.py:49
  136.9 7.9 %collective-permute-start.4 = (bf16[8,64,128]{2,1,0:T(8,128)(2,1)S(1)}, bf16[8,64,128]{2,1,0:T(8,128)(2,1)S(1)}, u32[]{:S(2)}, u32[]{:S(2)}) collective-permute-start(bf16[8,64,128]{2,1,0:T(8,128)(2,1)S(1)} %collective-permute-done.3), channel_id=1, source_target_pairs={{0,4},{4,8},{8,12},{12,16},{16,20},{20,24},{24,28},{28,0},{1,5},{5... | collective-permute-start | bytes 393224 | tf_op jit(solution)/shard_map/ppermute | solution.py:49
  144.7 11.7 %collective-permute-start.5 = (bf16[8,64,128]{2,1,0:T(8,128)(2,1)S(1)}, bf16[8,64,128]{2,1,0:T(8,128)(2,1)S(1)}, u32[]{:S(2)}, u32[]{:S(2)}) collective-permute-start(bf16[8,64,128]{2,1,0:T(8,128)(2,1)S(1)} %collective-permute-done.4), channel_id=1, source_target_pairs={{0,4},{4,8},{8,12},{12,16},{16,20},{20,24},{24,28},{28,0},{1,5},{5... | collective-permute-start | bytes 393224 | tf_op jit(solution)/shard_map/ppermute | solution.py:49
  156.4 7.7 %collective-permute-start.6 = (bf16[8,64,128]{2,1,0:T(8,128)(2,1)S(1)}, bf16[8,64,128]{2,1,0:T(8,128)(2,1)S(1)}, u32[]{:S(2)}, u32[]{:S(2)}) collective-permute-start(bf16[8,64,128]{2,1,0:T(8,128)(2,1)S(1)} %collective-permute-done.5), channel_id=1, source_target_pairs={{0,4},{4,8},{8,12},{12,16},{16,20},{20,24},{24,28},{28,0},{1,5},{5... | collective-permute-start | bytes 393224 | tf_op jit(solution)/shard_map/ppermute | solution.py:49
  173.9 6.4 %copy-start.5 = (bf16[64,64,256]{2,1,0:T(8,128)(2,1)S(1)}, bf16[64,64,256]{2,1,0:T(8,128)(2,1)}, u32[]{:S(2)}) copy-start(bf16[64,64,256]{2,1,0:T(8,128)(2,1)} %all-gather.3.cloned.1.call-done) | copy-start | bytes 6291460
  173.9 6.4 %copy-start.6 = (bf16[4096,128]{1,0:T(8,128)(2,1)S(1)}, bf16[4096,128]{1,0:T(8,128)(2,1)}, u32[]{:S(2)}) copy-start(bf16[4096,128]{1,0:T(8,128)(2,1)} %get-tuple-element.22) | copy-start | bytes 3145732
  195.5 4.8 %copy-start.3 = (bf16[64,128,256]{1,0,2:T(8,128)(2,1)S(1)}, bf16[64,128,256]{1,0,2:T(8,128)(2,1)}, u32[]{:S(2)}) copy-start(bf16[64,128,256]{1,0,2:T(8,128)(2,1)} %copy.20) | copy-start | bytes 12582916
  195.5 4.8 %copy-start.4 = (bf16[128,50,256]{0,1,2:T(8,128)(2,1)S(1)}, bf16[128,50,256]{0,1,2:T(8,128)(2,1)}, u32[]{:S(2)}) copy-start(bf16[128,50,256]{0,1,2:T(8,128)(2,1)} %copy.27) | copy-start | bytes 9830404
  200.3 40.4 %copy-start.7 = (bf16[128,50]{0,1:T(8,128)(2,1)S(1)}, bf16[128,50]{0,1:T(8,128)(2,1)}, u32[]{:S(2)}) copy-start(bf16[128,50]{0,1:T(8,128)(2,1)} %param.15) | copy-start | bytes 38404
  200.4 46.9 %copy-start.1 = (bf16[128,4096]{1,0:T(8,128)(2,1)S(1)}, bf16[128,4096]{1,0:T(8,128)(2,1)}, u32[]{:S(2)}) copy-start(bf16[128,4096]{1,0:T(8,128)(2,1)} %param.12) | copy-start | bytes 3145732
Sparse Core Ops, SparseCore 0:
  103.5 58.2 all-gather.2
  174.0 54.0 all-gather.4
